TPU v7x, 32 devices: a whole 2x2x4 slice. The times are simulated.
32 devices in a mesh: gx: 4 (over x, core), gy: 2 (over y), gz: 4 (over z).
Axes of the slice: x: 2, y: 2, z: 4, core: 2. Of those that a mesh axis runs over, the one named last changes fastest.
Arguments:
- coef: float32 [4, 64, 64, 512], P(None, 'gx', 'gy', 'gz'), may hold values from -6 to 6
- keep: int32 [4, 16, 16, 128], P(None, 'gx', 'gy', 'gz'), may hold values from 1 to 10
- courant: float32 [64, 64, 512], P('gx', 'gy', 'gz'), may hold values from 0.05 to 0.2
- damp: float32 [64, 64, 512], P('gx', 'gy', 'gz'), may hold values from 0 to 0.3
- adj_next: float32 [64, 64, 512], P('gx', 'gy', 'gz'), may hold values from -6 to 6
- adj_now: float32 [64, 64, 512], P('gx', 'gy', 'gz'), may hold values from -6 to 6
- rec_cell: int32 [4, 2, 4, 128], P('gx', 'gy', 'gz'), may hold values from 0 to 65535
- rec_data: float32 [4, 2, 4, 4, 128], P('gx', 'gy', 'gz'), may hold values from -6 to 6
Outputs:
- gradient: float32 [64, 64, 512], P('gx', 'gy', 'gz')
- adjoint_last: float32 [64, 64, 512], P('gx', 'gy', 'gz')
- adjoint_before: float32 [64, 64, 512], P('gx', 'gy', 'gz')
Inputs may be any that keep to these rules, and one draw needn't show every extreme that they name: `keep`: A block's coefficient (a, b, c) is kept when a + b + c is below this count. `rec_cell`: A row-major index into the 16 x 32 x 128 cells of the device's own block; indices may repeat.
All inputs are finite; a program needn't handle non-finite values.
Results may differ from a plain program's by a relative error of at most 0.00013.
Values sent between devices are 32-bit elements; how exact they have to be, the bound alone decides.
A program may use at most 64 MiB of HBM per device.

v0:
```python
import jax
import jax.numpy as jnp
from jax import lax
from jax.sharding import PartitionSpec as P

STAR = (-205.0 / 72.0, 8.0 / 5.0, -1.0 / 5.0, 8.0 / 315.0, -1.0 / 560.0)


def extended(value, sides, width):
    for axis, dim in sides:
        size, length = (lax.axis_size(axis), value.shape[dim])
        up = [(i, (i + 1) % size) for i in range(size - 1)]
        down = [(j, i) for i, j in up]
        last = lax.slice_in_dim(value, length - width, length, axis=dim)
        leading = lax.slice_in_dim(value, 0, width, axis=dim)
        before = lax.ppermute(last, axis, up)
        after = lax.ppermute(leading, axis, down)
        value = jnp.concatenate([before, value, after], axis=dim)
    return value


def dct_table():
    freq = jnp.arange(4, dtype=jnp.float32)[:, None]
    place = jnp.arange(4, dtype=jnp.float32)[None, :]
    scales = jnp.where(freq == 0.0, 0.5, jnp.sqrt(jnp.float32(0.5)))
    return scales * jnp.cos(jnp.pi * (2.0 * place + 1.0) * freq / 8.0)


def block_table(length):
    return jnp.kron(jnp.eye(length // 4, dtype=jnp.float32), dct_table())


def decode(block_coef, block_keep):
    size_x, size_y, size_z = block_coef.shape
    levels = (
        (jnp.arange(size_x, dtype=jnp.int32) % 4)[:, None, None]
        + (jnp.arange(size_y, dtype=jnp.int32) % 4)[None, :, None]
        + (jnp.arange(size_z, dtype=jnp.int32) % 4)[None, None, :]
    )
    spread = jnp.repeat(jnp.repeat(jnp.repeat(block_keep, 4, axis=0), 4, axis=1), 4, axis=2)
    masked = jnp.where(levels < spread, block_coef, 0.0)
    along_z = jnp.dot(
        masked.reshape(size_x * size_y, size_z),
        block_table(size_z),
        precision=lax.Precision.HIGHEST,
    ).reshape(size_x, size_y, size_z)
    along_y = jnp.einsum(
        "bj,ibk->ijk", block_table(size_y), along_z, precision=lax.Precision.HIGHEST
    )
    along_x = jnp.dot(
        block_table(size_x).T,
        along_y.reshape(size_x, size_y * size_z),
        precision=lax.Precision.HIGHEST,
    )
    return along_x.reshape(size_x, size_y, size_z)


def star_padded(padded, shape):
    size_x, size_y, size_z = shape
    total = 3.0 * STAR[0] * padded[4 : 4 + size_x, 4 : 4 + size_y, 4 : 4 + size_z]
    for reach in range(1, 5):
        plus_x = padded[4 + reach : 4 + reach + size_x, 4 : 4 + size_y, 4 : 4 + size_z]
        minus_x = padded[4 - reach : 4 - reach + size_x, 4 : 4 + size_y, 4 : 4 + size_z]
        plus_y = padded[4 : 4 + size_x, 4 + reach : 4 + reach + size_y, 4 : 4 + size_z]
        minus_y = padded[4 : 4 + size_x, 4 - reach : 4 - reach + size_y, 4 : 4 + size_z]
        plus_z = padded[4 : 4 + size_x, 4 : 4 + size_y, 4 + reach : 4 + reach + size_z]
        minus_z = padded[4 : 4 + size_x, 4 : 4 + size_y, 4 - reach : 4 - reach + size_z]
        total = total + STAR[reach] * (plus_x + minus_x + plus_y + minus_y + plus_z + minus_z)
    return total


def adjoint_laplace(field):
    padded = extended(field, (("gx", 0), ("gy", 1), ("gz", 2)), 4)
    return star_padded(padded, field.shape)


def local(coef, keep, courant, damp, adj_next, adj_now, rec_cell, rec_data):
    shape = adj_now.shape
    cells = shape[0] * shape[1] * shape[2]
    forwards = [decode(coef[step], keep[step]) for step in range(coef.shape[0])]
    stacked = jnp.stack(forwards)
    padded_all = extended(stacked, (("gx", 1), ("gy", 2), ("gz", 3)), 4)
    positions = rec_cell.reshape(-1)
    gradient = jnp.zeros(shape, jnp.float32)
    later = adj_next
    current = adj_now
    for step in range(coef.shape[0]):
        forward_lap = star_padded(padded_all[step], shape)
        gradient = gradient + courant * current * forward_lap
        inject = (
            jnp.zeros((cells,), jnp.float32)
            .at[positions]
            .add(rec_data[0, 0, 0, step])
            .reshape(shape)
        )
        earlier = (
            2.0 * current - (1.0 - damp) * later + courant * adjoint_laplace(current) + inject
        ) / (1.0 + damp)
        later = current
        current = earlier
    return (gradient, current, later)


def solution(mesh):
    in_specs = (
        P(None, "gx", "gy", "gz"),
        P(None, "gx", "gy", "gz"),
        P("gx", "gy", "gz"),
        P("gx", "gy", "gz"),
        P("gx", "gy", "gz"),
        P("gx", "gy", "gz"),
        P("gx", "gy", "gz", None),
        P("gx", "gy", "gz", None, None),
    )
    out_specs = (P("gx", "gy", "gz"), P("gx", "gy", "gz"), P("gx", "gy", "gz"))
    return jax.shard_map(local, mesh=mesh, in_specs=in_specs, out_specs=out_specs, check_vma=False)
```

profile of v0, /device:TPU:0, one launch (start us, length us, event | category | flops | bytes accessed | tf_op | source)
XLA Modules:
  0.0 206.1 jit_solution(10424516399267104764)
XLA Ops:
  3.1 2.4 %collective-permute-start.7 = (f32[4,32,128]{2,0,1:T(4,128)}, f32[4,32,128]{2,0,1:T(4,128)S(1)}, u32[]{:S(2)}, u32[]{:S(2)}) collective-permute-start(f32[4,32,128]{2,0,1:T(4,128)} %get-tuple-element.72), channel_id=1, source_target_pairs={{0,8},{8,16},{16,24},{1,9},{9,17},{17,25},{2,10},{10,18},{18,26},{... | collective-permute-start | bytes 196616 | tf_op jit(solution)/shard_map/ppermute | solution.py:16
  12.8 2.3 %copy.197 = f32[1,16,32,128]{2,1,3,0:T(8,128)} copy(f32[1,16,32,128]{3,2,1,0:T(8,128)} %get-tuple-element.28) | data formatting | bytes 524288
  38.2 4.5 %collective-permute-start.9 = (f32[24,4,128]{2,0,1:T(8,128)S(1)}, f32[24,4,128]{2,0,1:T(8,128)S(1)}, u32[]{:S(2)}, u32[]{:S(2)}) collective-permute-start(f32[24,4,128]{2,0,1:T(8,128)S(1)} %get-tuple-element.61), channel_id=1, source_target_pairs={{0,4},{1,5},{2,6},{3,7},{8,12},{9,13},{10,14},{11,15},{16,20},{17,... | collective-permute-start | bytes 147464 | tf_op jit(solution)/shard_map/ppermute | solution.py:16
  46.1 5.1 %collective-permute-start.11 = (f32[24,40,4]{2,0,1:T(8,128)S(1)}, f32[24,40,4]{2,0,1:T(8,128)S(1)}, u32[]{:S(2)}, u32[]{:S(2)}) collective-permute-start(f32[24,40,4]{2,0,1:T(8,128)S(1)} %get-tuple-element.46), channel_id=1, source_target_pairs={{0,1},{1,2},{2,3},{4,5},{5,6},{6,7},{8,9},{9,10},{10,11},{12,13},{... | collective-permute-start | bytes 46088 | tf_op jit(solution)/shard_map/ppermute | solution.py:16
  51.3 9.1 %collective-permute-done.10 = f32[24,40,4]{2,0,1:T(8,128)S(1)} collective-permute-done((f32[24,40,4]{2,0,1:T(8,128)S(1)}, f32[24,40,4]{2,0,1:T(8,128)S(1)}, u32[]{:S(2)}, u32[]{:S(2)}) %collective-permute-start.10) | collective-permute-done | bytes 15392 | tf_op jit(solution)/shard_map/ppermute | solution.py:17
  64.2 2.5 %collective-permute-start.13 = (f32[4,32,128]{2,0,1:T(4,128)S(1)}, f32[4,32,128]{2,0,1:T(4,128)S(1)}, u32[]{:S(2)}, u32[]{:S(2)}) collective-permute-start(f32[4,32,128]{2,0,1:T(4,128)S(1)} %get-tuple-element.68), channel_id=1, source_target_pairs={{0,8},{8,16},{16,24},{1,9},{9,17},{17,25},{2,10},{10,18},{18,26},{... | collective-permute-start | bytes 196616 | tf_op jit(solution)/shard_map/ppermute | solution.py:16
  71.5 4.5 %collective-permute-start.15 = (f32[24,4,128]{2,0,1:T(8,128)S(1)}, f32[24,4,128]{2,0,1:T(8,128)S(1)}, u32[]{:S(2)}, u32[]{:S(2)}) collective-permute-start(f32[24,4,128]{2,0,1:T(8,128)S(1)} %get-tuple-element.57), channel_id=1, source_target_pairs={{0,4},{1,5},{2,6},{3,7},{8,12},{9,13},{10,14},{11,15},{16,20},{17,... | collective-permute-start | bytes 147464 | tf_op jit(solution)/shard_map/ppermute | solution.py:16
  77.4 4.9 %collective-permute-start = (f32[4,4,32,128]{3,1,2,0:T(4,128)S(1)}, f32[4,4,32,128]{3,1,2,0:T(4,128)S(1)}, u32[]{:S(2)}, u32[]{:S(2)}) collective-permute-start(f32[4,4,32,128]{3,1,2,0:T(4,128)S(1)} %get-tuple-element.25), channel_id=1, source_target_pairs={{0,8},{8,16},{16,24},{1,9},{9,17},{17,25},{2,10},{10,18},{18,26},{... | collective-permute-start | bytes 786440 | tf_op jit(solution)/shard_map/ppermute | solution.py:16
  85.4 5.2 %collective-permute-start.17 = (f32[24,40,4]{2,0,1:T(8,128)S(1)}, f32[24,40,4]{2,0,1:T(8,128)S(1)}, u32[]{:S(2)}, u32[]{:S(2)}) collective-permute-start(f32[24,40,4]{2,0,1:T(8,128)S(1)} %get-tuple-element.42), channel_id=1, source_target_pairs={{0,1},{1,2},{2,3},{4,5},{5,6},{6,7},{8,9},{9,10},{10,11},{12,13},{... | collective-permute-start | bytes 46088 | tf_op jit(solution)/shard_map/ppermute | solution.py:16
  90.7 8.8 %collective-permute-done.16 = f32[24,40,4]{2,0,1:T(8,128)S(1)} collective-permute-done((f32[24,40,4]{2,0,1:T(8,128)S(1)}, f32[24,40,4]{2,0,1:T(8,128)S(1)}, u32[]{:S(2)}, u32[]{:S(2)}) %collective-permute-start.16) | collective-permute-done | bytes 15392 | tf_op jit(solution)/shard_map/ppermute | solution.py:17
  104.5 3.4 %collective-permute-start.19 = (f32[4,32,128]{2,0,1:T(4,128)S(1)}, f32[4,32,128]{2,0,1:T(4,128)S(1)}, u32[]{:S(2)}, u32[]{:S(2)}) collective-permute-start(f32[4,32,128]{2,0,1:T(4,128)S(1)} %get-tuple-element.65), channel_id=1, source_target_pairs={{0,8},{8,16},{16,24},{1,9},{9,17},{17,25},{2,10},{10,18},{18,26},{... | collective-permute-start | bytes 196616 | tf_op jit(solution)/shard_map/ppermute | solution.py:16
  111.3 4.5 %collective-permute-start.21 = (f32[24,4,128]{2,0,1:T(8,128)S(1)}, f32[24,4,128]{2,0,1:T(8,128)S(1)}, u32[]{:S(2)}, u32[]{:S(2)}) collective-permute-start(f32[24,4,128]{2,0,1:T(8,128)S(1)} %get-tuple-element.53), channel_id=1, source_target_pairs={{0,4},{1,5},{2,6},{3,7},{8,12},{9,13},{10,14},{11,15},{16,20},{17,... | collective-permute-start | bytes 147464 | tf_op jit(solution)/shard_map/ppermute | solution.py:16
  117.3 4.6 %collective-permute-start.2 = (f32[4,24,4,128]{3,1,2,0:T(8,128)S(1)}, f32[4,24,4,128]{3,1,2,0:T(8,128)S(1)}, u32[]{:S(2)}, u32[]{:S(2)}) collective-permute-start(f32[4,24,4,128]{3,1,2,0:T(8,128)S(1)} %get-tuple-element.23), channel_id=1, source_target_pairs={{0,4},{1,5},{2,6},{3,7},{8,12},{9,13},{10,14},{11,15},{16,20},{17,... | collective-permute-start | bytes 589832 | tf_op jit(solution)/shard_map/ppermute | solution.py:16
  124.4 5.5 %collective-permute-start.23 = (f32[24,40,4]{2,0,1:T(8,128)}, f32[24,40,4]{2,0,1:T(8,128)}, u32[]{:S(2)}, u32[]{:S(2)}) collective-permute-start(f32[24,40,4]{2,0,1:T(8,128)} %get-tuple-element.38), channel_id=1, source_target_pairs={{0,1},{1,2},{2,3},{4,5},{5,6},{6,7},{8,9},{9,10},{10,11},{12,13},{... | collective-permute-start | bytes 46088 | tf_op jit(solution)/shard_map/ppermute | solution.py:16
  134.4 3.0 %copy.159 = f32[4,24,40,4]{2,1,3,0:T(8,128)} copy(f32[4,24,40,4]{3,1,2,0:T(8,128)} %get-tuple-element.22) | data formatting | bytes 122880 | tf_op jit(solution)/shard_map/slice | solution.py:15
  140.3 5.2 %collective-permute-start.4 = (f32[4,24,40,4]{2,1,3,0:T(8,128)}, f32[4,24,40,4]{2,1,3,0:T(8,128)}, u32[]{:S(2)}, u32[]{:S(2)}) collective-permute-start(f32[4,24,40,4]{2,1,3,0:T(8,128)} %copy.158), channel_id=1, source_target_pairs={{0,1},{1,2},{2,3},{4,5},{5,6},{6,7},{8,9},{9,10},{10,11},{12,13},{... | collective-permute-start | bytes 184328 | tf_op jit(solution)/shard_map/ppermute | solution.py:16
  145.5 3.1 %pad_maximum_fusion.4 = (f32[24,40,132]{2,0,1:T(8,128)}, f32[24,40,132]{2,0,1:T(8,128)}) fusion(f32[24,40,4]{2,0,1:T(8,128)} %collective-permute-done.22, f32[24,4,128]{2,0,1:T(8,128)} %copy-done.20, f32[4,32,128]{2,0,1:T(4,128)} %copy-done.13, f32[16,32,128]{2,0,1:T(8,128)S(1)} %fusion.84, f32[4,32,128]{2,0,1:T(4,128)} %copy-done.15, ...), kind=kLoop, calls=%fused_computation.35 | loop fusion | flops 1267200 | bytes 1536000 | tf_op jit(solution)/shard_map/concatenate | solution.py:18
  150.3 2.9 %copy.160 = f32[4,24,40,4]{3,1,2,0:T(8,128)} copy(f32[4,24,40,4]{2,1,3,0:T(8,128)} %collective-permute-done.4) | data formatting | bytes 122880 | tf_op jit(solution)/shard_map/ppermute | solution.py:16
  153.3 7.2 %pad_maximum_fusion = f32[4,24,40,136]{3,1,2,0:T(8,128)S(1)} fusion(f32[4,24,40,4]{3,1,2,0:T(8,128)S(1)} %copy.161, f32[4,24,4,128]{3,1,2,0:T(8,128)} %copy-done.18, f32[4,4,32,128]{3,1,2,0:T(4,128)} %copy-done.11, f32[1,16,32,128]{3,1,2,0:T(8,128)S(1)} %convolution_bitcast_fusion, f32[1,16,32,128]{3,1,2,0:T(8,128)S(1)} %convolution_bitcast_fusion.1, ...), kind=kLoop, calls=%fused_computation.4 | loop fusion | flops 4700160 | bytes 4177920 | tf_op jit(solution)/shard_map/concatenate | solution.py:18
  162.6 7.7 %fusion.146 = (f32[16,32,128]{2,0,1:T(8,128)S(1)}, f32[16,32,128]{2,0,1:T(8,128)S(1)}) fusion(f32[24,40,136]{2,0,1:T(8,128)S(1)} %get-tuple-element.18, f32[24,40,136]{2,0,1:T(8,128)S(1)} %get-tuple-element.19, f32[24,40,136]{2,0,1:T(8,128)S(1)} %get-tuple-element.20, f32[24,40,136]{2,0,1:T(8,128)S(1)} %get-tuple-element.17, f32[16,32,128]{2,0,1:T(8,128)S(1)} %fusion.84, ...), kind=kLoop, calls=%fused_computation.242 | loop fusion | flops 11337728 | bytes 32636928 | tf_op jit(solution)/shard_map/add | solution.py:89
  173.3 4.9 %collective-permute-done.24 = f32[4,32,128]{2,0,1:T(4,128)S(1)} collective-permute-done((f32[4,32,128]{2,0,1:T(4,128)S(1)}, f32[4,32,128]{2,0,1:T(4,128)S(1)}, u32[]{:S(2)}, u32[]{:S(2)}) %collective-permute-start.24) | collective-permute-done | bytes 65568 | tf_op jit(solution)/shard_map/ppermute | solution.py:17
  179.5 4.5 %collective-permute-start.27 = (f32[24,4,128]{2,0,1:T(8,128)S(1)}, f32[24,4,128]{2,0,1:T(8,128)S(1)}, u32[]{:S(2)}, u32[]{:S(2)}) collective-permute-start(f32[24,4,128]{2,0,1:T(8,128)S(1)} %get-tuple-element.49), channel_id=1, source_target_pairs={{0,4},{1,5},{2,6},{3,7},{8,12},{9,13},{10,14},{11,15},{16,20},{17,... | collective-permute-start | bytes 147464 | tf_op jit(solution)/shard_map/ppermute | solution.py:16
  188.6 4.6 %collective-permute-start.29 = (f32[24,40,4]{2,0,1:T(8,128)S(1)}, f32[24,40,4]{2,0,1:T(8,128)S(1)}, u32[]{:S(2)}, u32[]{:S(2)}) collective-permute-start(f32[24,40,4]{2,0,1:T(8,128)S(1)} %get-tuple-element.34), channel_id=1, source_target_pairs={{0,1},{1,2},{2,3},{4,5},{5,6},{6,7},{8,9},{9,10},{10,11},{12,13},{... | collective-permute-start | bytes 46088 | tf_op jit(solution)/shard_map/ppermute | solution.py:16
  193.3 8.6 %collective-permute-done.28 = f32[24,40,4]{2,0,1:T(8,128)S(1)} collective-permute-done((f32[24,40,4]{2,0,1:T(8,128)S(1)}, f32[24,40,4]{2,0,1:T(8,128)S(1)}, u32[]{:S(2)}, u32[]{:S(2)}) %collective-permute-start.28) | collective-permute-done | bytes 15392 | tf_op jit(solution)/shard_map/ppermute | solution.py:17
  (190 shorter events, 85.2 us)
Async XLA Ops:
  3.1 33.7 %collective-permute-start.7 = (f32[4,32,128]{2,0,1:T(4,128)}, f32[4,32,128]{2,0,1:T(4,128)S(1)}, u32[]{:S(2)}, u32[]{:S(2)}) collective-permute-start(f32[4,32,128]{2,0,1:T(4,128)} %get-tuple-element.72), channel_id=1, source_target_pairs={{0,8},{8,16},{16,24},{1,9},{9,17},{17,25},{2,10},{10,18},{18,26},{... | collective-permute-start | bytes 196616 | tf_op jit(solution)/shard_map/ppermute | solution.py:16
  5.5 31.4 %collective-permute-start.6 = (f32[4,32,128]{2,0,1:T(4,128)}, f32[4,32,128]{2,0,1:T(4,128)S(1)}, u32[]{:S(2)}, u32[]{:S(2)}) collective-permute-start(f32[4,32,128]{2,0,1:T(4,128)} %get-tuple-element.71), channel_id=1, source_target_pairs={{8,0},{16,8},{24,16},{9,1},{17,9},{25,17},{10,2},{18,10},{26,18},{... | collective-permute-start | bytes 196616 | tf_op jit(solution)/shard_map/ppermute | solution.py:17
  38.2 6.3 %collective-permute-start.9 = (f32[24,4,128]{2,0,1:T(8,128)S(1)}, f32[24,4,128]{2,0,1:T(8,128)S(1)}, u32[]{:S(2)}, u32[]{:S(2)}) collective-permute-start(f32[24,4,128]{2,0,1:T(8,128)S(1)} %get-tuple-element.61), channel_id=1, source_target_pairs={{0,4},{1,5},{2,6},{3,7},{8,12},{9,13},{10,14},{11,15},{16,20},{17,... | collective-permute-start | bytes 147464 | tf_op jit(solution)/shard_map/ppermute | solution.py:16
  44.8 15.6 %collective-permute-start.10 = (f32[24,40,4]{2,0,1:T(8,128)S(1)}, f32[24,40,4]{2,0,1:T(8,128)S(1)}, u32[]{:S(2)}, u32[]{:S(2)}) collective-permute-start(f32[24,40,4]{2,0,1:T(8,128)S(1)} %get-tuple-element.45), channel_id=1, source_target_pairs={{1,0},{2,1},{3,2},{5,4},{6,5},{7,6},{9,8},{10,9},{11,10},{13,12},{... | collective-permute-start | bytes 46088 | tf_op jit(solution)/shard_map/ppermute | solution.py:17
  46.1 16.2 %collective-permute-start.11 = (f32[24,40,4]{2,0,1:T(8,128)S(1)}, f32[24,40,4]{2,0,1:T(8,128)S(1)}, u32[]{:S(2)}, u32[]{:S(2)}) collective-permute-start(f32[24,40,4]{2,0,1:T(8,128)S(1)} %get-tuple-element.46), channel_id=1, source_target_pairs={{0,1},{1,2},{2,3},{4,5},{5,6},{6,7},{8,9},{9,10},{10,11},{12,13},{... | collective-permute-start | bytes 46088 | tf_op jit(solution)/shard_map/ppermute | solution.py:16
  70.2 13.6 %collective-permute-start.14 = (f32[24,4,128]{2,0,1:T(8,128)S(1)}, f32[24,4,128]{2,0,1:T(8,128)S(1)}, u32[]{:S(2)}, u32[]{:S(2)}) collective-permute-start(f32[24,4,128]{2,0,1:T(8,128)S(1)} %get-tuple-element.58), channel_id=1, source_target_pairs={{4,0},{5,1},{6,2},{7,3},{12,8},{13,9},{14,10},{15,11},{20,16},{21,... | collective-permute-start | bytes 147464 | tf_op jit(solution)/shard_map/ppermute | solution.py:17
  71.5 12.4 %collective-permute-start.15 = (f32[24,4,128]{2,0,1:T(8,128)S(1)}, f32[24,4,128]{2,0,1:T(8,128)S(1)}, u32[]{:S(2)}, u32[]{:S(2)}) collective-permute-start(f32[24,4,128]{2,0,1:T(8,128)S(1)} %get-tuple-element.57), channel_id=1, source_target_pairs={{0,4},{1,5},{2,6},{3,7},{8,12},{9,13},{10,14},{11,15},{16,20},{17,... | collective-permute-start | bytes 147464 | tf_op jit(solution)/shard_map/ppermute | solution.py:16
  76.1 39.8 %collective-permute-start.1 = (f32[4,4,32,128]{3,1,2,0:T(4,128)S(1)}, f32[4,4,32,128]{3,1,2,0:T(4,128)S(1)}, u32[]{:S(2)}, u32[]{:S(2)}) collective-permute-start(f32[4,4,32,128]{3,1,2,0:T(4,128)S(1)} %get-tuple-element.26), channel_id=1, source_target_pairs={{8,0},{16,8},{24,16},{9,1},{17,9},{25,17},{10,2},{18,10},{26,18},{... | collective-permute-start | bytes 786440 | tf_op jit(solution)/shard_map/ppermute | solution.py:17
  77.4 38.5 %collective-permute-start = (f32[4,4,32,128]{3,1,2,0:T(4,128)S(1)}, f32[4,4,32,128]{3,1,2,0:T(4,128)S(1)}, u32[]{:S(2)}, u32[]{:S(2)}) collective-permute-start(f32[4,4,32,128]{3,1,2,0:T(4,128)S(1)} %get-tuple-element.25), channel_id=1, source_target_pairs={{0,8},{8,16},{16,24},{1,9},{9,17},{17,25},{2,10},{10,18},{18,26},{... | collective-permute-start | bytes 786440 | tf_op jit(solution)/shard_map/ppermute | solution.py:16
  84.1 15.4 %collective-permute-start.16 = (f32[24,40,4]{2,0,1:T(8,128)S(1)}, f32[24,40,4]{2,0,1:T(8,128)S(1)}, u32[]{:S(2)}, u32[]{:S(2)}) collective-permute-start(f32[24,40,4]{2,0,1:T(8,128)S(1)} %get-tuple-element.41), channel_id=1, source_target_pairs={{1,0},{2,1},{3,2},{5,4},{6,5},{7,6},{9,8},{10,9},{11,10},{13,12},{... | collective-permute-start | bytes 46088 | tf_op jit(solution)/shard_map/ppermute | solution.py:17
  85.4 16.0 %collective-permute-start.17 = (f32[24,40,4]{2,0,1:T(8,128)S(1)}, f32[24,40,4]{2,0,1:T(8,128)S(1)}, u32[]{:S(2)}, u32[]{:S(2)}) collective-permute-start(f32[24,40,4]{2,0,1:T(8,128)S(1)} %get-tuple-element.42), channel_id=1, source_target_pairs={{0,1},{1,2},{2,3},{4,5},{5,6},{6,7},{8,9},{9,10},{10,11},{12,13},{... | collective-permute-start | bytes 46088 | tf_op jit(solution)/shard_map/ppermute | solution.py:16
  103.2 6.8 %collective-permute-start.18 = (f32[4,32,128]{2,0,1:T(4,128)S(1)}, f32[4,32,128]{2,0,1:T(4,128)S(1)}, u32[]{:S(2)}, u32[]{:S(2)}) collective-permute-start(f32[4,32,128]{2,0,1:T(4,128)S(1)} %get-tuple-element.66), channel_id=1, source_target_pairs={{8,0},{16,8},{24,16},{9,1},{17,9},{25,17},{10,2},{18,10},{26,18},{... | collective-permute-start | bytes 196616 | tf_op jit(solution)/shard_map/ppermute | solution.py:17
  110.0 11.8 %collective-permute-start.20 = (f32[24,4,128]{2,0,1:T(8,128)S(1)}, f32[24,4,128]{2,0,1:T(8,128)S(1)}, u32[]{:S(2)}, u32[]{:S(2)}) collective-permute-start(f32[24,4,128]{2,0,1:T(8,128)S(1)} %get-tuple-element.54), channel_id=1, source_target_pairs={{4,0},{5,1},{6,2},{7,3},{12,8},{13,9},{14,10},{15,11},{20,16},{21,... | collective-permute-start | bytes 147464 | tf_op jit(solution)/shard_map/ppermute | solution.py:17
  111.3 10.6 %collective-permute-start.21 = (f32[24,4,128]{2,0,1:T(8,128)S(1)}, f32[24,4,128]{2,0,1:T(8,128)S(1)}, u32[]{:S(2)}, u32[]{:S(2)}) collective-permute-start(f32[24,4,128]{2,0,1:T(8,128)S(1)} %get-tuple-element.53), channel_id=1, source_target_pairs={{0,4},{1,5},{2,6},{3,7},{8,12},{9,13},{10,14},{11,15},{16,20},{17,... | collective-permute-start | bytes 147464 | tf_op jit(solution)/shard_map/ppermute | solution.py:16
  116.0 14.9 %collective-permute-start.3 = (f32[4,24,4,128]{3,1,2,0:T(8,128)S(1)}, f32[4,24,4,128]{3,1,2,0:T(8,128)S(1)}, u32[]{:S(2)}, u32[]{:S(2)}) collective-permute-start(f32[4,24,4,128]{3,1,2,0:T(8,128)S(1)} %get-tuple-element.24), channel_id=1, source_target_pairs={{4,0},{5,1},{6,2},{7,3},{12,8},{13,9},{14,10},{15,11},{20,16},{21,... | collective-permute-start | bytes 589832 | tf_op jit(solution)/shard_map/ppermute | solution.py:17
  117.3 13.6 %collective-permute-start.2 = (f32[4,24,4,128]{3,1,2,0:T(8,128)S(1)}, f32[4,24,4,128]{3,1,2,0:T(8,128)S(1)}, u32[]{:S(2)}, u32[]{:S(2)}) collective-permute-start(f32[4,24,4,128]{3,1,2,0:T(8,128)S(1)} %get-tuple-element.23), channel_id=1, source_target_pairs={{0,4},{1,5},{2,6},{3,7},{8,12},{9,13},{10,14},{11,15},{16,20},{17,... | collective-permute-start | bytes 589832 | tf_op jit(solution)/shard_map/ppermute | solution.py:16
  123.1 22.4 %collective-permute-start.22 = (f32[24,40,4]{2,0,1:T(8,128)}, f32[24,40,4]{2,0,1:T(8,128)}, u32[]{:S(2)}, u32[]{:S(2)}) collective-permute-start(f32[24,40,4]{2,0,1:T(8,128)} %get-tuple-element.37), channel_id=1, source_target_pairs={{1,0},{2,1},{3,2},{5,4},{6,5},{7,6},{9,8},{10,9},{11,10},{13,12},{... | collective-permute-start | bytes 46088 | tf_op jit(solution)/shard_map/ppermute | solution.py:17
  124.4 21.2 %collective-permute-start.23 = (f32[24,40,4]{2,0,1:T(8,128)}, f32[24,40,4]{2,0,1:T(8,128)}, u32[]{:S(2)}, u32[]{:S(2)}) collective-permute-start(f32[24,40,4]{2,0,1:T(8,128)} %get-tuple-element.38), channel_id=1, source_target_pairs={{0,1},{1,2},{2,3},{4,5},{5,6},{6,7},{8,9},{9,10},{10,11},{12,13},{... | collective-permute-start | bytes 46088 | tf_op jit(solution)/shard_map/ppermute | solution.py:16
  137.4 11.3 %collective-permute-start.5 = (f32[4,24,40,4]{2,1,3,0:T(8,128)}, f32[4,24,40,4]{2,1,3,0:T(8,128)}, u32[]{:S(2)}, u32[]{:S(2)}) collective-permute-start(f32[4,24,40,4]{2,1,3,0:T(8,128)} %copy.159), channel_id=1, source_target_pairs={{1,0},{2,1},{3,2},{5,4},{6,5},{7,6},{9,8},{10,9},{11,10},{13,12},{... | collective-permute-start | bytes 184328 | tf_op jit(solution)/shard_map/ppermute | solution.py:17
  140.3 10.0 %collective-permute-start.4 = (f32[4,24,40,4]{2,1,3,0:T(8,128)}, f32[4,24,40,4]{2,1,3,0:T(8,128)}, u32[]{:S(2)}, u32[]{:S(2)}) collective-permute-start(f32[4,24,40,4]{2,1,3,0:T(8,128)} %copy.158), channel_id=1, source_target_pairs={{0,1},{1,2},{2,3},{4,5},{5,6},{6,7},{8,9},{9,10},{10,11},{12,13},{... | collective-permute-start | bytes 184328 | tf_op jit(solution)/shard_map/ppermute | solution.py:16
  178.2 8.9 %collective-permute-start.26 = (f32[24,4,128]{2,0,1:T(8,128)S(1)}, f32[24,4,128]{2,0,1:T(8,128)S(1)}, u32[]{:S(2)}, u32[]{:S(2)}) collective-permute-start(f32[24,4,128]{2,0,1:T(8,128)S(1)} %get-tuple-element.50), channel_id=1, source_target_pairs={{4,0},{5,1},{6,2},{7,3},{12,8},{13,9},{14,10},{15,11},{20,16},{21,... | collective-permute-start | bytes 147464 | tf_op jit(solution)/shard_map/ppermute | solution.py:17
  179.5 7.6 %collective-permute-start.27 = (f32[24,4,128]{2,0,1:T(8,128)S(1)}, f32[24,4,128]{2,0,1:T(8,128)S(1)}, u32[]{:S(2)}, u32[]{:S(2)}) collective-permute-start(f32[24,4,128]{2,0,1:T(8,128)S(1)} %get-tuple-element.49), channel_id=1, source_target_pairs={{0,4},{1,5},{2,6},{3,7},{8,12},{9,13},{10,14},{11,15},{16,20},{17,... | collective-permute-start | bytes 147464 | tf_op jit(solution)/shard_map/ppermute | solution.py:16
  187.4 14.6 %collective-permute-start.28 = (f32[24,40,4]{2,0,1:T(8,128)S(1)}, f32[24,40,4]{2,0,1:T(8,128)S(1)}, u32[]{:S(2)}, u32[]{:S(2)}) collective-permute-start(f32[24,40,4]{2,0,1:T(8,128)S(1)} %get-tuple-element.33), channel_id=1, source_target_pairs={{1,0},{2,1},{3,2},{5,4},{6,5},{7,6},{9,8},{10,9},{11,10},{13,12},{... | collective-permute-start | bytes 46088 | tf_op jit(solution)/shard_map/ppermute | solution.py:17
  188.6 15.0 %collective-permute-start.29 = (f32[24,40,4]{2,0,1:T(8,128)S(1)}, f32[24,40,4]{2,0,1:T(8,128)S(1)}, u32[]{:S(2)}, u32[]{:S(2)}) collective-permute-start(f32[24,40,4]{2,0,1:T(8,128)S(1)} %get-tuple-element.34), channel_id=1, source_target_pairs={{0,1},{1,2},{2,3},{4,5},{5,6},{6,7},{8,9},{9,10},{10,11},{12,13},{... | collective-permute-start | bytes 46088 | tf_op jit(solution)/shard_map/ppermute | solution.py:16
  (33 other events, 227.1 us)
where the time goes:
time: 209 us; the launch traced here: 206 us
  starting transfers between devices  82.8 us (40%)
  waiting for transfers between devices  40.5 us (19%)
  local copies, waits for them, and re-layouts  36 us (17%)
  other arithmetic  34 us (16%)
  matrix products  11.2 us (5%)
    ppermute x15, starting transfers between devices, extended(): before = lax.ppermute(last, axis, up)  63.2 us
    ppermute x15, waiting for transfers between devices, extended(): after = lax.ppermute(leading, axis, down)  33.3 us
    ppermute x15, starting transfers between devices, extended(): after = lax.ppermute(leading, axis, down)  19.6 us
    concatenate x18, other arithmetic, extended(): value = jnp.concatenate([before, value, after], axis=dim)  13.5 us
    unnamed x62, local copies, waits for them, and re-layouts  13 us
    add x1, other arithmetic, local(): gradient = gradient + courant * current * forward_lap  7.68 us
    dot_general x4, matrix products, decode(): jnp.dot(masked.reshape(size_x * size_y, size_z), block_table(size_z), pre...  7.6 us
    ppermute x15, waiting for transfers between devices, extended(): before = lax.ppermute(last, axis, up)  7.16 us
  transfers between devices with their start and end apart: 30, of which 10 were waited for; matrix products, arithmetic and copies ran while one was open for 26% of the time, Pallas kernels for 0%

commit v1 on v0

v1 whole, which is shorter than its diff:
```python
import functools

import jax
import jax.numpy as jnp
import numpy as np
from jax import lax
from jax.experimental import pallas as pl
from jax.experimental.pallas import tpu as pltpu
from jax.sharding import PartitionSpec as P

STAR = (-205.0 / 72.0, 8.0 / 5.0, -1.0 / 5.0, 8.0 / 315.0, -1.0 / 560.0)
MESH = pl.DeviceIdType.MESH
F32, BF16 = jnp.float32, jnp.bfloat16
AXES = ("gx", "gy", "gz")
PADX, PADY = 4, 8


def halves_np(table):
    high = table.astype(jnp.bfloat16)
    low = (table - high.astype(np.float32)).astype(jnp.bfloat16)
    return high, low


def tables(size_y, size_z):
    freq, place = np.arange(4)[:, None], np.arange(4)[None, :]
    scale = np.where(freq == 0, 0.5, np.sqrt(0.5))
    dct = scale * np.cos(np.pi * (2.0 * place + 1.0) * freq / 8.0)
    dz = np.kron(np.eye(size_z // 4), dct).astype(np.float32)
    dxy = np.kron(dct, np.kron(np.eye(size_y // 4), dct)).T.astype(np.float32)
    taps = {k: STAR[k] for k in range(1, 5)}
    inner = np.zeros((size_z, size_z), np.float32)
    halo = np.zeros((8, size_z), np.float32)
    for lane in range(size_z):
        for k, c in taps.items():
            for at in (lane + k, lane - k):
                if 0 <= at < size_z:
                    inner[at, lane] += c
                elif at < 0:
                    halo[4 + at, lane] += c
                else:
                    halo[4 + at - size_z, lane] += c
    pick = np.zeros((8, size_z), np.float32)
    for j in range(4):
        pick[j, j] = 1.0
        pick[4 + j, size_z - 4 + j] = 1.0
    dz_h, dz_l = halves_np(dz)
    dxy_h, dxy_l = halves_np(dxy)
    in_h, in_l = halves_np(inner)
    ha_h, ha_l = halves_np(halo)
    pick = pick.astype(jnp.bfloat16)
    spread = np.kron(np.eye(size_z // 4), np.ones((1, 4))).astype(jnp.bfloat16)
    repeat = np.kron(np.eye(size_y // 4), np.ones((4, 1)))
    return (
        np.concatenate([dz_h, dz_h, dz_l], 0),
        np.concatenate([dxy_h, dxy_h, dxy_l], 1),
        np.concatenate([in_h, in_h, in_l], 0),
        np.concatenate([ha_h, ha_h, ha_l, 0 * ha_l], 0),
        np.concatenate([pick, pick], 1),
        spread,
        repeat,
    )


def halves(value):
    high = value.astype(BF16)
    low = (value - high.astype(F32)).astype(BF16)
    return high, low


def dot(a, b, dims=((1,), (0,))):
    return lax.dot_general(a, b, (dims, ((), ())), preferred_element_type=F32)


def kernel(shape, steps, ntab, *refs):
    size_x, size_y, size_z = shape
    rows = size_x * size_y
    groups = size_x // 4
    ins, refs = refs[:8 + ntab], refs[8 + ntab:]
    outs, refs = refs[:3], refs[3:]
    vins, refs = refs[:8 + ntab], refs[8 + ntab:]
    (F, X, Y, ZS, ZR, Z, J, INV, B, A, G, T, LAST, LF, isem, osem, ssem, rsem) = refs
    coef_v, keep_v, cour_v, damp_v, next_v, _, cell_v, data_v = vins[:8]
    dz_v, dxy_v, in_v, ha_v, pick_v, spread_v, repeat_v = vins[8:]
    pos = [lax.axis_index(a) for a in AXES]
    num = [lax.axis_size(a) for a in AXES]
    below = [p > 0 for p in pos]
    above = [p < n - 1 for p, n in zip(pos, num)]
    body = (pl.ds(PADX, size_x), pl.ds(PADY, size_y))

    order = [5, 3, 2, 4] + list(range(8, 8 + ntab)) + [6, 7, 1, 0]
    loads = {}
    for i in order:
        dst = F.at[(0,) + body] if i == 5 else vins[i]
        loads[i] = pltpu.make_async_copy(ins[i], dst, isem.at[i])
        loads[i].start()

    barrier = pltpu.get_barrier_semaphore()
    total = jnp.int32(0)
    for d, axis in enumerate(AXES):
        for has, to in ((above[d], pos[d] + 1), (below[d], pos[d] - 1)):
            total = total + has.astype(jnp.int32)

            @pl.when(has)
            def _(axis=axis, to=to):
                pl.semaphore_signal(barrier, inc=1, device_id={axis: to}, device_id_type=MESH)

    F[:, :, pl.ds(0, PADY), :] = jnp.zeros((2 * steps, size_x + 8, PADY, size_z), F32)
    F[:, :, pl.ds(PADY + size_y, PADY), :] = jnp.zeros((2 * steps, size_x + 8, PADY, size_z), F32)
    F[:, pl.ds(0, PADX), pl.ds(PADY, size_y), :] = jnp.zeros((2 * steps, PADX, size_y, size_z), F32)
    F[:, pl.ds(PADX + size_x, PADX), pl.ds(PADY, size_y), :] = jnp.zeros((2 * steps, PADX, size_y, size_z), F32)
    Y[:, 0, :, pl.ds(8, 8), :] = jnp.zeros((2 * steps, size_x, 8, size_z), F32)
    Y[:, 1, :, pl.ds(0, 8), :] = jnp.zeros((2 * steps, size_x, 8, size_z), F32)
    for side, has in ((0, below), (1, above)):

        @pl.when(jnp.logical_not(has[0]))
        def _(side=side):
            X[:, side] = jnp.zeros((2 * steps, 4, size_y, size_z), F32)

        @pl.when(jnp.logical_not(has[1]))
        def _(side=side):
            Y[:, side, :, pl.ds(4 + 4 * side, 4), :] = jnp.zeros((2 * steps, size_x, 4, size_z), F32)

        @pl.when(jnp.logical_not(has[2]))
        def _(side=side):
            ZR[:, side] = jnp.zeros((2 * steps, 4, rows), F32)

    def copy_of(r, d):
        axis, up = AXES[d // 2], d % 2 == 0
        if d == 0:
            src, dst = F.at[r, pl.ds(PADX + size_x - 4, 4), pl.ds(PADY, size_y)], X.at[r, 0]
        elif d == 1:
            src, dst = F.at[r, pl.ds(PADX, 4), pl.ds(PADY, size_y)], X.at[r, 1]
        elif d == 2:
            src = F.at[r, pl.ds(PADX, size_x), pl.ds(PADY + size_y - 4, 4)]
            dst = Y.at[r, 0, :, pl.ds(4, 4)]
        elif d == 3:
            src, dst = F.at[r, pl.ds(PADX, size_x), pl.ds(PADY, 4)], Y.at[r, 1, :, pl.ds(8, 4)]
        elif d == 4:
            src, dst = ZS.at[r, 1], ZR.at[r, 0]
        else:
            src, dst = ZS.at[r, 0], ZR.at[r, 1]
        to = pos[d // 2] + (1 if up else -1)
        return pltpu.make_async_remote_copy(
            src_ref=src, dst_ref=dst, send_sem=ssem.at[r, d], recv_sem=rsem.at[r, d],
            device_id={axis: to}, device_id_type=MESH,
        )

    def goes(d):
        return above[d // 2] if d % 2 == 0 else below[d // 2]

    def comes(d):
        return below[d // 2] if d % 2 == 0 else above[d // 2]

    def send(r, ds):
        for d in ds:

            @pl.when(goes(d))
            def _(d=d):
                copy_of(r, d).start()

    def arrive(r):
        for d in range(6):

            @pl.when(comes(d))
            def _(d=d):
                copy_of(r, d).wait_recv()

    def split_field(r):
        parts = [F[r, PADX + x, pl.ds(PADY, size_y), :] for x in range(size_x)]
        return halves(jnp.concatenate(parts, 0))

    def pack(r, high, low):
        packed = dot(pick_v[...], jnp.concatenate([high, low], 1), ((1,), (1,)))
        ZS[r, 0] = packed[0:4]
        ZS[r, 1] = packed[4:8]

    def inner_z(high, low):
        Z[...] = dot(jnp.concatenate([high, low, high], 1), in_v[...])

    def planes(fun, unit=2):
        def trip(i, carry):
            for j in range(unit):
                fun(i * unit + j)
            return carry

        lax.fori_loop(0, size_x // unit, trip, 0)

    def star(r, x):
        centre = pl.ds(PADY, size_y)
        out = 3.0 * STAR[0] * F[r, PADX + x, centre, :]
        for k in range(1, 5):
            out += STAR[k] * (
                (F[r, PADX + x + k, centre, :] + F[r, PADX + x - k, centre, :])
                + (F[r, PADX + x, pl.ds(PADY + k, size_y), :] + F[r, PADX + x, pl.ds(PADY - k, size_y), :])
            )
        return out + Z[pl.ds(pl.multiple_of(x * size_y, size_y), size_y), :]

    def halo_z(r):
        high, low = halves(jnp.concatenate([ZR[r, 0], ZR[r, 1]], 0).T)
        stacked = jnp.concatenate([high, low, high, jnp.zeros_like(low)], 1)
        Z[...] = dot(stacked, ha_v[...])

    def halo(r, x):
        out = Z[pl.ds(x * size_y, size_y), :]
        for k in range(1, 5):
            if x - k < 0:
                out += STAR[k] * X[r, 0, 4 + x - k]
            if x + k >= size_x:
                out += STAR[k] * X[r, 1, x + k - size_x]
        first = sum(STAR[k] * Y[r, 0, x, pl.ds(8 - k, 8), :] for k in range(1, 5))
        final = sum(STAR[k] * Y[r, 1, x, pl.ds(k, 8), :] for k in range(1, 5))
        return jnp.concatenate([out[0:8] + first, out[8:size_y - 8], out[size_y - 8:] + final], 0)

    cell = []

    def inject(s):
        if not cell:
            loads[6].wait()
            loads[7].wait()
        shift = size_z.bit_length() - 1
        at = cell_v[...]
        row = lax.shift_right_logical(at, jnp.full_like(at, shift))
        lane = at & (size_z - 1)
        hot = jnp.where(lax.broadcasted_iota(jnp.int32, (size_z, at.shape[1]), 0) == lane, 1.0, 0.0).astype(BF16)
        cell.append(1)
        spot = jnp.where(lax.broadcasted_iota(jnp.int32, (rows, at.shape[1]), 0) == row, data_v[pl.ds(s, 1), :], 0.0)
        high, low = halves(spot)
        J[...] = dot(jnp.concatenate([high, low], 1), jnp.concatenate([hot, hot], 1), ((1,), (1,)))

    def before_halo(s):
        def one(x):
            lap = star(s, x)
            later = next_v[x] if s == 0 else F[s - 1, PADX + x, pl.ds(PADY, size_y), :]
            got = J[pl.ds(pl.multiple_of(x * size_y, size_y), size_y), :]
            value = 2.0 * F[s, PADX + x, pl.ds(PADY, size_y), :] - (1.0 - damp_v[x]) * later + got
            A[x] = INV[x] * value + B[x] * lap

        planes(one)

    def after_halo(s):
        halo_z(s)
        for x in range(size_x):
            value = A[x] + B[x] * halo(s, x)
            if s == steps - 1:
                LAST[x] = value
            else:
                F[s + 1, PADX + x, pl.ds(PADY, size_y), :] = value

    def mask_setup():
        loads[1].wait()
        wide = dot(keep_v[...].astype(F32).astype(BF16), spread_v[...])
        sub = lax.broadcasted_iota(jnp.int32, (size_y, size_z), 0) % 4
        lan = lax.broadcasted_iota(jnp.int32, (size_y, size_z), 1) % 4
        level = (sub + lan).astype(F32)
        per = size_y // 4
        for g in range(steps * groups):
            T[g] = dot(repeat_v[...], wide[g * per:(g + 1) * per].astype(BF16)) - level

    def decode(s):
        r = steps + s
        parts = []
        for g in range(groups):
            limit = T[s * groups + g]
            for a in range(4):
                block = coef_v[s, g * 4 + a]
                parts.append(jnp.where(limit > float(a), block, 0.0))
        high, low = halves(jnp.concatenate(parts, 0))
        along = dot(jnp.concatenate([high, low, high], 1), dz_v[...])
        high, low = halves(along)
        span = 4 * size_y
        hs = jnp.concatenate([high[g * span:(g + 1) * span] for g in range(groups)], 1)
        ls = jnp.concatenate([low[g * span:(g + 1) * span] for g in range(groups)], 1)
        out = dot(dxy_v[...], jnp.concatenate([hs, ls, hs], 0))
        for g in range(groups):
            for a in range(4):
                F[r, PADX + 4 * g + a, pl.ds(PADY, size_y), :] = out[
                    a * size_y:(a + 1) * size_y, g * size_z:(g + 1) * size_z
                ]
        send(r, (0, 1, 2, 3))
        pack(r, *split_field(r))
        send(r, (4, 5))

    def gradient(s):
        r = steps + s
        inner_z(*split_field(r))

        def one(x):
            LF[x] = star(r, x)

        planes(one)
        arrive(r)
        halo_z(r)
        for x in range(size_x):
            term = cour_v[x] * F[s, PADX + x, pl.ds(PADY, size_y), :] * (LF[x] + halo(r, x))
            G[x] = term if s == 0 else G[x] + term

    def setup_scales():
        loads[2].wait()
        loads[3].wait()

        def one(x):
            inverse = 1.0 / (1.0 + damp_v[x])
            INV[x] = inverse
            B[x] = cour_v[x] * inverse

        planes(one)

    for i in (5,) + tuple(range(8, 8 + ntab)):
        loads[i].wait()
    high, low = split_field(0)
    pack(0, high, low)
    pl.semaphore_wait(barrier, total)
    send(0, range(6))
    writes = []
    for s in range(steps):
        inner_z(high, low)
        inject(s)
        if s == 0:
            setup_scales()
            loads[4].wait()
        before_halo(s)
        if s == 0:
            mask_setup()
            loads[0].wait()
        for t in (2 * s, 2 * s + 1):
            if t < steps:
                decode(t)
            elif t < 2 * steps:
                gradient(t - steps)
        if s == steps - 1:
            writes.append(pltpu.make_async_copy(F.at[(s,) + body], outs[2], osem.at[2]))
            writes.append(pltpu.make_async_copy(G, outs[0], osem.at[0]))
            for w in writes:
                w.start()
        arrive(s)
        after_halo(s)
        if s < steps - 1:
            send(s + 1, (0, 1, 2, 3))
            high, low = split_field(s + 1)
            pack(s + 1, high, low)
            send(s + 1, (4, 5))
    writes.append(pltpu.make_async_copy(LAST, outs[1], osem.at[1]))
    writes[-1].start()
    for r in range(2 * steps):
        for d in range(6):

            @pl.when(goes(d))
            def _(r=r, d=d):
                copy_of(r, d).wait_send()
    for w in writes:
        w.wait()


def local(coef, keep, courant, damp, adj_next, adj_now, rec_cell, rec_data):
    shape = adj_now.shape
    size_x, size_y, size_z = shape
    steps = coef.shape[0]
    rows = size_x * size_y
    args = [
        coef, keep.reshape(-1, keep.shape[-1]), courant, damp, adj_next, adj_now,
        rec_cell.reshape(1, -1), rec_data.reshape(steps, -1),
    ]
    tabs = list(tables(size_y, size_z))
    tabs[-1] = tabs[-1].astype(jnp.bfloat16)
    tabs = [jnp.asarray(t) for t in tabs]
    args += tabs
    box = pltpu.VMEM(shape, F32)
    flat = pltpu.VMEM((rows, size_z), F32)
    scratch = [pltpu.VMEM(a.shape, a.dtype) for a in args]
    scratch[5] = pltpu.VMEM((8, 128), F32)
    scratch += [
        pltpu.VMEM((2 * steps, size_x + 8, size_y + 16, size_z), F32),
        pltpu.VMEM((2 * steps, 2, 4, size_y, size_z), F32),
        pltpu.VMEM((2 * steps, 2, size_x, 16, size_z), F32),
        pltpu.VMEM((2 * steps, 2, 4, rows), F32),
        pltpu.VMEM((2 * steps, 2, 4, rows), F32),
        flat, flat, box, box, box, box,
        pltpu.VMEM((steps * size_x // 4, size_y, size_z), F32),
        box, box,
        pltpu.SemaphoreType.DMA((len(args),)),
        pltpu.SemaphoreType.DMA((3,)),
        pltpu.SemaphoreType.DMA((2 * steps, 6)),
        pltpu.SemaphoreType.DMA((2 * steps, 6)),
    ]
    hbm = pl.BlockSpec(memory_space=pl.ANY)
    return tuple(pl.pallas_call(
        functools.partial(kernel, shape, steps, len(tabs)),
        out_shape=[jax.ShapeDtypeStruct(shape, F32)] * 3,
        in_specs=[hbm] * len(args),
        out_specs=[hbm] * 3,
        scratch_shapes=scratch,
        compiler_params=pltpu.CompilerParams(
            collective_id=0, has_side_effects=True, vmem_limit_bytes=48 * 2**20
        ),
    )(*args))


def solution(mesh):
    in_specs = (
        P(None, "gx", "gy", "gz"),
        P(None, "gx", "gy", "gz"),
        P("gx", "gy", "gz"),
        P("gx", "gy", "gz"),
        P("gx", "gy", "gz"),
        P("gx", "gy", "gz"),
        P("gx", "gy", "gz", None),
        P("gx", "gy", "gz", None, None),
    )
    out_specs = (P("gx", "gy", "gz"), P("gx", "gy", "gz"), P("gx", "gy", "gz"))
    return jax.shard_map(local, mesh=mesh, in_specs=in_specs, out_specs=out_specs, check_vma=False)
```

time: 209 us -> 34.2 us (0.16); the launches traced: 206 us -> 33.6 us
  starting transfers between devices: 82.8 us -> 0 us
  waiting for transfers between devices: 40.5 us -> 0 us
  other arithmetic: 34 us -> 0 us
  local copies, waits for them, and re-layouts: 36 us -> 12.7 us
  Pallas kernels: 0 us -> 20.2 us
  matrix products: 11.2 us -> 0 us
    ppermute x30 -> x0, starting transfers between devices: 82.8 us -> none  [the longest x15 63.2 us: extended(): before = lax.ppermute(last, axis, up)]
    ppermute x30 -> x0, waiting for transfers between devices: 40.5 us -> none  [the longest x15 33.3 us: extended(): after = lax.ppermute(leading, axis, down)]
    pallas_call x0 -> x1, Pallas kernels: none -> 20.2 us  [local(): pl.pallas_call(functools.partial(kernel, shape, steps, len(tabs)), out_sh...]
    concatenate x18 -> x0, other arithmetic: 13.5 us -> none  [extended(): value = jnp.concatenate([before, value, after], axis=dim)]
    dot_general x12 -> x0, matrix products: 11.2 us -> none  [the longest x4 7.6 us: decode(): jnp.dot(masked.reshape(size_x * size_y, size_z), block_table(size_z), pre...]
    slice x12 -> x0, local copies, waits for them, and re-layouts: 10.8 us -> none  [the longest x8 5.34 us: extended(): leading = lax.slice_in_dim(value, 0, width, axis=dim)]
    add x2 -> x0, other arithmetic: 7.76 us -> none  [the longest x1 7.68 us: local(): gradient = gradient + courant * current * forward_lap]
    scatter-add x4 -> x0, other arithmetic: 6.27 us -> none  [local(): inject = jnp.zeros((cells,), jnp.float32).at[positions].add(rec_data[0, 0...]
  transfers between devices with their start and end apart: 30 -> 0, of which waited for: 10 -> 0; matrix products, arithmetic and copies ran while one was open for 26% -> 0% of each run, Pallas kernels for 0% -> 0%
where the time goes in v1:
time: 34.2 us; the launch traced here: 33.6 us
  Pallas kernels  20.2 us (59%)
  local copies, waits for them, and re-layouts  12.7 us (37%)
  between operations  0.69 us (2%)
    pallas_call x1, Pallas kernels, local(): pl.pallas_call(functools.partial(kernel, shape, steps, len(tabs)), out_sh...  20.2 us
    unnamed x33, local copies, waits for them, and re-layouts  12.7 us

profile of v1, /device:TPU:0, one launch (start us, length us, event | category | flops | bytes accessed | tf_op | source)
XLA Modules:
  0.0 33.6 jit_solution(4925965506252389757)
XLA Ops:
  0.6 0.0 copy-start.9
  0.6 0.0 copy-start.12
  0.7 0.0 copy-start.13
  0.7 0.0 copy-start.14
  0.7 0.7 %copy-done.9 = bf16[32,8]{1,0:T(8,128)(2,1)S(1)} copy-done((bf16[32,8]{1,0:T(8,128)(2,1)S(1)}, bf16[32,8]{1,0:T(8,128)(2,1)}, u32[]{:S(2)}) %copy-start.9) | copy-done | bytes 536
  1.3 0.0 copy-done.12
  1.3 0.0 copy-done.13
  1.4 0.0 copy-done.14
  1.4 0.0 copy-start
  1.4 1.2 %copy-done = f32[4,16,32,128]{3,2,1,0:T(8,128)S(1)} copy-done((f32[4,16,32,128]{3,2,1,0:T(8,128)S(1)}, f32[4,16,32,128]{3,2,1,0:T(8,128)}, u32[]{:S(2)}) %copy-start) | copy-done | bytes 1048600
  2.6 0.9 %copy-done.1 = f32[16,32,128]{2,1,0:T(8,128)S(1)} copy-done((f32[16,32,128]{2,1,0:T(8,128)S(1)}, f32[16,32,128]{2,1,0:T(8,128)}, u32[]{:S(2)}) %copy-start.1) | copy-done | bytes 262168
  3.5 0.9 %copy-done.2 = f32[16,32,128]{2,1,0:T(8,128)S(1)} copy-done((f32[16,32,128]{2,1,0:T(8,128)S(1)}, f32[16,32,128]{2,1,0:T(8,128)}, u32[]{:S(2)}) %copy-start.2) | copy-done | bytes 262168
  4.5 0.9 %copy-done.3 = f32[16,32,128]{2,1,0:T(8,128)S(1)} copy-done((f32[16,32,128]{2,1,0:T(8,128)S(1)}, f32[16,32,128]{2,1,0:T(8,128)}, u32[]{:S(2)}) %copy-start.3) | copy-done | bytes 262168
  5.4 0.9 %copy-done.4 = f32[16,32,128]{2,1,0:T(8,128)S(1)} copy-done((f32[16,32,128]{2,1,0:T(8,128)S(1)}, f32[16,32,128]{2,1,0:T(8,128)}, u32[]{:S(2)}) %copy-start.4) | copy-done | bytes 262168
  6.4 0.9 %copy-done.5 = bf16[384,128]{1,0:T(8,128)(2,1)S(1)} copy-done((bf16[384,128]{1,0:T(8,128)(2,1)S(1)}, bf16[384,128]{1,0:T(8,128)(2,1)}, u32[]{:S(2)}) %copy-start.5) | copy-done | bytes 98328
  7.3 0.9 %copy-done.6 = bf16[128,384]{1,0:T(8,128)(2,1)S(1)} copy-done((bf16[128,384]{1,0:T(8,128)(2,1)S(1)}, bf16[128,384]{1,0:T(8,128)(2,1)}, u32[]{:S(2)}) %copy-start.6) | copy-done | bytes 98328
  8.2 0.9 %copy-done.7 = bf16[384,128]{1,0:T(8,128)(2,1)S(1)} copy-done((bf16[384,128]{1,0:T(8,128)(2,1)S(1)}, bf16[384,128]{1,0:T(8,128)(2,1)}, u32[]{:S(2)}) %copy-start.7) | copy-done | bytes 98328
  9.1 0.8 %copy-done.8 = s32[4,4,8,32]{3,2,1,0:T(8,128)S(1)} copy-done((s32[4,4,8,32]{3,2,1,0:T(8,128)S(1)}, s32[4,4,8,32]{3,2,1,0:T(8,128)}, u32[]{:S(2)}) %copy-start.8) | copy-done | bytes 16408
  9.9 0.7 %copy-done.10 = bf16[32,128]{1,0:T(8,128)(2,1)S(1)} copy-done((bf16[32,128]{1,0:T(8,128)(2,1)S(1)}, bf16[32,128]{1,0:T(8,128)(2,1)}, u32[]{:S(2)}) %copy-start.10) | copy-done | bytes 8216
  10.6 0.7 %copy-done.11 = bf16[32,128]{1,0:T(8,128)(2,1)S(1)} copy-done((bf16[32,128]{1,0:T(8,128)(2,1)S(1)}, bf16[32,128]{1,0:T(8,128)(2,1)}, u32[]{:S(2)}) %copy-start.11) | copy-done | bytes 8216
  11.3 20.2 %shard_map.166 = (f32[16,32,128]{2,1,0:T(8,128)S(1)}, f32[16,32,128]{2,1,0:T(8,128)S(1)}, f32[16,32,128]{2,1,0:T(8,128)S(1)}) custom-call(f32[4,16,32,128]{3,2,1,0:T(8,128)S(1)} %copy-done, s32[128,32]{1,0:T(8,128)S(1)} %bitcast.3, f32[16,32,128]{2,1,0:T(8,128)S(1)} %copy-done.1, f32[16,32,128]{2,1,0:T(8,128)S(1)} %copy-done.2, ...), custom_call_target="tpu_custom_call" | custom-call | tf_op jit(solution)/shard_map/pallas_call | solution.py:386
  31.5 0.7 %copy.21 = f32[16,32,128]{2,1,0:T(8,128)} copy(f32[16,32,128]{2,1,0:T(8,128)S(1)} %get-tuple-element.6) | data formatting | bytes 524288
  32.2 0.7 %copy.22 = f32[16,32,128]{2,1,0:T(8,128)} copy(f32[16,32,128]{2,1,0:T(8,128)S(1)} %get-tuple-element.7) | data formatting | bytes 524288
  32.9 0.7 %copy.23 = f32[16,32,128]{2,1,0:T(8,128)} copy(f32[16,32,128]{2,1,0:T(8,128)S(1)} %get-tuple-element.8) | data formatting | bytes 524288
  (10 shorter events, 0.0 us)
Async XLA Ops:
  0.6 0.7 %copy-start.9 = (bf16[32,8]{1,0:T(8,128)(2,1)S(1)}, bf16[32,8]{1,0:T(8,128)(2,1)}, u32[]{:S(2)}) copy-start(bf16[32,8]{1,0:T(8,128)(2,1)} %constant.20.clone.refs_14_) | copy-start | bytes 1540
  0.6 0.7 %copy-start.12 = (bf16[8,256]{1,0:T(8,128)(2,1)S(1)}, bf16[8,256]{1,0:T(8,128)(2,1)}, u32[]{:S(2)}) copy-start(bf16[8,256]{1,0:T(8,128)(2,1)} %constant.18.clone.refs_12_) | copy-start | bytes 12292
  0.7 0.7 %copy-start.13 = (f32[1,1,1,4,128]{4,3,2,1,0:T(4,128)S(1)}, f32[1,1,1,4,128]{4,3,2,1,0:T(4,128)}, u32[]{:S(2)}) copy-start(f32[1,1,1,4,128]{4,3,2,1,0:T(4,128)} %param.22) | copy-start | bytes 6148
  0.7 0.7 %copy-start.14 = (s32[1,1,1,128]{3,2,1,0:T(1,128)S(1)}, s32[1,1,1,128]{3,2,1,0:T(1,128)}, u32[]{:S(2)}) copy-start(s32[1,1,1,128]{3,2,1,0:T(1,128)} %param.21) | copy-start | bytes 1540
  1.4 1.2 %copy-start = (f32[4,16,32,128]{3,2,1,0:T(8,128)S(1)}, f32[4,16,32,128]{3,2,1,0:T(8,128)}, u32[]{:S(2)}) copy-start(f32[4,16,32,128]{3,2,1,0:T(8,128)} %refs_0_.1) | copy-start | bytes 3145732
  2.6 0.9 %copy-start.1 = (f32[16,32,128]{2,1,0:T(8,128)S(1)}, f32[16,32,128]{2,1,0:T(8,128)}, u32[]{:S(2)}) copy-start(f32[16,32,128]{2,1,0:T(8,128)} %refs_2_.1) | copy-start | bytes 786436
  3.5 0.9 %copy-start.2 = (f32[16,32,128]{2,1,0:T(8,128)S(1)}, f32[16,32,128]{2,1,0:T(8,128)}, u32[]{:S(2)}) copy-start(f32[16,32,128]{2,1,0:T(8,128)} %refs_3_.1) | copy-start | bytes 786436
  4.5 0.9 %copy-start.3 = (f32[16,32,128]{2,1,0:T(8,128)S(1)}, f32[16,32,128]{2,1,0:T(8,128)}, u32[]{:S(2)}) copy-start(f32[16,32,128]{2,1,0:T(8,128)} %refs_4_.1) | copy-start | bytes 786436
  5.4 0.9 %copy-start.4 = (f32[16,32,128]{2,1,0:T(8,128)S(1)}, f32[16,32,128]{2,1,0:T(8,128)}, u32[]{:S(2)}) copy-start(f32[16,32,128]{2,1,0:T(8,128)} %refs_5_.1) | copy-start | bytes 786436
  6.4 0.9 %copy-start.5 = (bf16[384,128]{1,0:T(8,128)(2,1)S(1)}, bf16[384,128]{1,0:T(8,128)(2,1)}, u32[]{:S(2)}) copy-start(bf16[384,128]{1,0:T(8,128)(2,1)} %constant.16.clone.refs_10_) | copy-start | bytes 294916
  7.3 0.9 %copy-start.6 = (bf16[128,384]{1,0:T(8,128)(2,1)S(1)}, bf16[128,384]{1,0:T(8,128)(2,1)}, u32[]{:S(2)}) copy-start(bf16[128,384]{1,0:T(8,128)(2,1)} %constant.15.clone.refs_9_) | copy-start | bytes 294916
  8.2 0.9 %copy-start.7 = (bf16[384,128]{1,0:T(8,128)(2,1)S(1)}, bf16[384,128]{1,0:T(8,128)(2,1)}, u32[]{:S(2)}) copy-start(bf16[384,128]{1,0:T(8,128)(2,1)} %constant.14.clone.refs_8_) | copy-start | bytes 294916
  9.1 0.8 %copy-start.8 = (s32[4,4,8,32]{3,2,1,0:T(8,128)S(1)}, s32[4,4,8,32]{3,2,1,0:T(8,128)}, u32[]{:S(2)}) copy-start(s32[4,4,8,32]{3,2,1,0:T(8,128)} %param.16) | copy-start | bytes 49156
  9.9 0.7 %copy-start.10 = (bf16[32,128]{1,0:T(8,128)(2,1)S(1)}, bf16[32,128]{1,0:T(8,128)(2,1)}, u32[]{:S(2)}) copy-start(bf16[32,128]{1,0:T(8,128)(2,1)} %constant.19.clone.refs_13_) | copy-start | bytes 24580
  10.6 0.7 %copy-start.11 = (bf16[32,128]{1,0:T(8,128)(2,1)S(1)}, bf16[32,128]{1,0:T(8,128)(2,1)}, u32[]{:S(2)}) copy-start(bf16[32,128]{1,0:T(8,128)(2,1)} %constant.17.clone.refs_11_) | copy-start | bytes 24580

commit v2 on v1

--- a/solution.py
+++ b/solution.py
@@ -78,7 +78,8 @@
     ins, refs = refs[:8 + ntab], refs[8 + ntab:]
     outs, refs = refs[:3], refs[3:]
     vins, refs = refs[:8 + ntab], refs[8 + ntab:]
-    (F, X, Y, ZS, ZR, Z, J, INV, B, A, G, T, LAST, LF, isem, osem, ssem, rsem) = refs
+    (F, X, Y, ZS, ZR, Z, J, INV, B, A, T, LF, isem, ssem, rsem) = refs
+    G, LAST, BEFORE = outs
     coef_v, keep_v, cour_v, damp_v, next_v, _, cell_v, data_v = vins[:8]
     dz_v, dxy_v, in_v, ha_v, pick_v, spread_v, repeat_v = vins[8:]
     pos = [lax.axis_index(a) for a in AXES]
@@ -245,6 +246,8 @@
                 LAST[x] = value
             else:
                 F[s + 1, PADX + x, pl.ds(PADY, size_y), :] = value
+            if s == steps - 2:
+                BEFORE[x] = value
 
     def mask_setup():
         loads[1].wait()
@@ -311,7 +314,6 @@
     pack(0, high, low)
     pl.semaphore_wait(barrier, total)
     send(0, range(6))
-    writes = []
     for s in range(steps):
         inner_z(high, low)
         inject(s)
@@ -327,11 +329,6 @@
                 decode(t)
             elif t < 2 * steps:
                 gradient(t - steps)
-        if s == steps - 1:
-            writes.append(pltpu.make_async_copy(F.at[(s,) + body], outs[2], osem.at[2]))
-            writes.append(pltpu.make_async_copy(G, outs[0], osem.at[0]))
-            for w in writes:
-                w.start()
         arrive(s)
         after_halo(s)
         if s < steps - 1:
@@ -339,16 +336,21 @@
             high, low = split_field(s + 1)
             pack(s + 1, high, low)
             send(s + 1, (4, 5))
-    writes.append(pltpu.make_async_copy(LAST, outs[1], osem.at[1]))
-    writes[-1].start()
     for r in range(2 * steps):
         for d in range(6):
 
             @pl.when(goes(d))
             def _(r=r, d=d):
                 copy_of(r, d).wait_send()
-    for w in writes:
-        w.wait()
+
+
+def flush(*refs):
+    sources, targets, sem = refs[:3], refs[3:6], refs[6]
+    copies = [pltpu.make_async_copy(a, b, sem.at[i]) for i, (a, b) in enumerate(zip(sources, targets))]
+    for c in copies:
+        c.start()
+    for c in copies:
+        c.wait()
 
 
 def local(coef, keep, courant, damp, adj_next, adj_now, rec_cell, rec_data):
@@ -374,25 +376,33 @@
         pltpu.VMEM((2 * steps, 2, size_x, 16, size_z), F32),
         pltpu.VMEM((2 * steps, 2, 4, rows), F32),
         pltpu.VMEM((2 * steps, 2, 4, rows), F32),
-        flat, flat, box, box, box, box,
+        flat, flat, box, box, box,
         pltpu.VMEM((steps * size_x // 4, size_y, size_z), F32),
-        box, box,
+        box,
         pltpu.SemaphoreType.DMA((len(args),)),
-        pltpu.SemaphoreType.DMA((3,)),
         pltpu.SemaphoreType.DMA((2 * steps, 6)),
         pltpu.SemaphoreType.DMA((2 * steps, 6)),
     ]
     hbm = pl.BlockSpec(memory_space=pl.ANY)
-    return tuple(pl.pallas_call(
+    args = [pltpu.with_memory_space_constraint(a, pltpu.HBM) for a in args]
+    results = pl.pallas_call(
         functools.partial(kernel, shape, steps, len(tabs)),
         out_shape=[jax.ShapeDtypeStruct(shape, F32)] * 3,
         in_specs=[hbm] * len(args),
-        out_specs=[hbm] * 3,
+        out_specs=[pl.BlockSpec(memory_space=pltpu.VMEM)] * 3,
         scratch_shapes=scratch,
         compiler_params=pltpu.CompilerParams(
             collective_id=0, has_side_effects=True, vmem_limit_bytes=48 * 2**20
         ),
-    )(*args))
+    )(*args)
+    return tuple(pl.pallas_call(
+        flush,
+        out_shape=[jax.ShapeDtypeStruct(shape, F32)] * 3,
+        in_specs=[hbm] * 3,
+        out_specs=[hbm] * 3,
+        scratch_shapes=[pltpu.SemaphoreType.DMA((3,))],
+        compiler_params=pltpu.CompilerParams(vmem_limit_bytes=2**20),
+    )(*results))
 
 
 def solution(mesh):

time: 34.2 us -> 21.4 us (0.63); the launches traced: 33.6 us -> 21.2 us
  local copies, waits for them, and re-layouts: 12.7 us -> 0 us
  Pallas kernels: 20.2 us -> 20.6 us
    unnamed x33 -> x0, local copies, waits for them, and re-layouts: 12.7 us -> none
    pallas_call x0 -> x1, Pallas kernels: none -> 0.9 us  [local(): pl.pallas_call(flush, out_shape=[jax.ShapeDtypeStruct(shape, F32)] * 3, i...]
    pallas_call x1, Pallas kernels: 20.2 us -> 19.7 us  [local(): pl.pallas_call(functools.partial(kernel, shape, steps, len(tabs)), out_sh...]
where the time goes in v2:
time: 21.4 us; the launch traced here: 21.2 us
  Pallas kernels  20.6 us (96%)
  between operations  0.64 us (3%)
    pallas_call x1, Pallas kernels, local(): pl.pallas_call(functools.partial(kernel, shape, steps, len(tabs)), out_sh...  19.7 us
    pallas_call x1, Pallas kernels, local(): pl.pallas_call(flush, out_shape=[jax.ShapeDtypeStruct(shape, F32)] * 3, i...  0.9 us

profile of v2, /device:TPU:0, one launch (start us, length us, event | category | flops | bytes accessed | tf_op | source)
XLA Modules:
  0.0 21.2 jit_solution(11123013605049143251)
XLA Ops:
  0.6 19.7 %shard_map.166 = (f32[16,32,128]{2,1,0:T(8,128)S(1)}, f32[16,32,128]{2,1,0:T(8,128)S(1)}, f32[16,32,128]{2,1,0:T(8,128)S(1)}) custom-call(f32[4,16,32,128]{3,2,1,0:T(8,128)} %refs_0_.1, s32[128,32]{1,0:T(8,128)} %bitcast.3, f32[16,32,128]{2,1,0:T(8,128)} %refs_2_.1, f32[16,32,128]{2,1,0:T(8,128)} %refs_3_.1, f32[16,32,128]{2,1,0:T(8,128)} %refs_4_.1, ...), custom_call_target="tpu_custom_call" | custom-call | tf_op jit(solution)/shard_map/pallas_call | solution.py:388
  20.3 0.9 %shard_map.167 = (f32[16,32,128]{2,1,0:T(8,128)}, f32[16,32,128]{2,1,0:T(8,128)}, f32[16,32,128]{2,1,0:T(8,128)}) custom-call(f32[16,32,128]{2,1,0:T(8,128)S(1)} %get-tuple-element.6.refs_0_, f32[16,32,128]{2,1,0:T(8,128)S(1)} %get-tuple-element.7.refs_1_, f32[16,32,128]{2,1,0:T(8,128)S(1)} %get-tuple-element.8.refs_2_), custom_call_target="tpu_custom_call" | custom-call | tf_op jit(solution)/shard_map/pallas_call | solution.py:398

commit v3 on v2

--- a/solution.py
+++ b/solution.py
@@ -159,8 +159,8 @@
             def _(d=d):
                 copy_of(r, d).start()
 
-    def arrive(r):
-        for d in range(6):
+    def arrive(r, ds=range(6)):
+        for d in ds:
 
             @pl.when(comes(d))
             def _(d=d):
@@ -197,9 +197,10 @@
         return out + Z[pl.ds(pl.multiple_of(x * size_y, size_y), size_y), :]
 
     def halo_z(r):
-        high, low = halves(jnp.concatenate([ZR[r, 0], ZR[r, 1]], 0).T)
-        stacked = jnp.concatenate([high, low, high, jnp.zeros_like(low)], 1)
-        Z[...] = dot(stacked, ha_v[...])
+        faces = jnp.concatenate([ZR[r, 0], ZR[r, 1]], 0)
+        high = faces.astype(BF16).astype(F32)
+        stacked = jnp.concatenate([high, faces - high, high, jnp.zeros_like(high)], 0)
+        Z[...] = dot(stacked.astype(BF16), ha_v[...], ((0,), (0,)))
 
     def halo(r, x):
         out = Z[pl.ds(x * size_y, size_y), :]
@@ -239,7 +240,9 @@
         planes(one)
 
     def after_halo(s):
+        arrive(s, (4, 5))
         halo_z(s)
+        arrive(s, (0, 1, 2, 3))
         for x in range(size_x):
             value = A[x] + B[x] * halo(s, x)
             if s == steps - 1:
@@ -329,13 +332,11 @@
                 decode(t)
             elif t < 2 * steps:
                 gradient(t - steps)
-        arrive(s)
         after_halo(s)
         if s < steps - 1:
-            send(s + 1, (0, 1, 2, 3))
             high, low = split_field(s + 1)
             pack(s + 1, high, low)
-            send(s + 1, (4, 5))
+            send(s + 1, range(6))
     for r in range(2 * steps):
         for d in range(6):
 

time: 21.4 us -> 20.5 us (0.958)
  Pallas kernels: 20.6 us -> 19.7 us
    pallas_call x1, Pallas kernels: 19.7 us -> 18.8 us  [local(): pl.pallas_call(functools.partial(kernel, shape, steps, len(tabs)), out_sh...]
where the time goes in v3:
time: 20.5 us; the launch traced here: 20.3 us
  Pallas kernels  19.7 us (96%)
  between operations  0.64 us (3%)
    pallas_call x1, Pallas kernels, local(): pl.pallas_call(functools.partial(kernel, shape, steps, len(tabs)), out_sh...  18.8 us
    pallas_call x1, Pallas kernels, local(): pl.pallas_call(flush, out_shape=[jax.ShapeDtypeStruct(shape, F32)] * 3, i...  0.9 us

profile of v3, /device:TPU:0, one launch (start us, length us, event | category | flops | bytes accessed | tf_op | source)
XLA Modules:
  0.0 20.3 jit_solution(14120865219776310884)
XLA Ops:
  0.6 18.8 %shard_map.166 = (f32[16,32,128]{2,1,0:T(8,128)S(1)}, f32[16,32,128]{2,1,0:T(8,128)S(1)}, f32[16,32,128]{2,1,0:T(8,128)S(1)}) custom-call(f32[4,16,32,128]{3,2,1,0:T(8,128)} %refs_0_.1, s32[128,32]{1,0:T(8,128)} %bitcast.3, f32[16,32,128]{2,1,0:T(8,128)} %refs_2_.1, f32[16,32,128]{2,1,0:T(8,128)} %refs_3_.1, f32[16,32,128]{2,1,0:T(8,128)} %refs_4_.1, ...), custom_call_target="tpu_custom_call" | custom-call | tf_op jit(solution)/shard_map/pallas_call | solution.py:389
  19.4 0.9 %shard_map.167 = (f32[16,32,128]{2,1,0:T(8,128)}, f32[16,32,128]{2,1,0:T(8,128)}, f32[16,32,128]{2,1,0:T(8,128)}) custom-call(f32[16,32,128]{2,1,0:T(8,128)S(1)} %get-tuple-element.6.refs_0_, f32[16,32,128]{2,1,0:T(8,128)S(1)} %get-tuple-element.7.refs_1_, f32[16,32,128]{2,1,0:T(8,128)S(1)} %get-tuple-element.8.refs_2_), custom_call_target="tpu_custom_call" | custom-call | tf_op jit(solution)/shard_map/pallas_call | solution.py:399
